TPU v7x, 32 devices: a whole 2x2x4 slice. The times are simulated.
32 devices in a mesh: dp: 8 (over y, x, core), tensor: 4 (over z).
Axes of the slice: x: 2, y: 2, z: 4, core: 2. Of those that a mesh axis runs over, the one named last changes fastest.
Arguments:
- tokens_in: bfloat16 [8192, 1024], P(('dp', 'tensor')), may hold values from -6 to 6
- starts: int32 [8, 4], P('dp'), may hold values from 0 to 768, as said below
- ln1_gain: float32 [1024], P(('dp', 'tensor')), may hold values from 0.25 to 1.75
- ln1_bias: float32 [1024], P(('dp', 'tensor')), may hold values from -4 to 4
- w_qkv: bfloat16 [1024, 3072], P('dp', 'tensor'), may hold values from -0.25 to 0.25
- b_qv: bfloat16 [128, 16], P('tensor', 'dp'), may hold values from -6 to 6
- w_out: bfloat16 [1024, 1024], P('tensor', 'dp'), may hold values from -0.75 to 0.75
- b_out: float32 [1024], P(('dp', 'tensor')), may hold values from -6 to 6
- ln2_gain: float32 [1024], P(('dp', 'tensor')), may hold values from 0.25 to 1.75
- ln2_bias: float32 [1024], P(('dp', 'tensor')), may hold values from -4 to 4
- w_up: bfloat16 [1024, 4096], P('dp', 'tensor'), may hold values from -0.1875 to 0.1875
- b_up: bfloat16 [256, 16], P('tensor', 'dp'), may hold values from -6 to 6
- w_down: bfloat16 [4096, 1024], P('tensor', 'dp'), may hold values from -0.09375 to 0.09375
- b_down: float32 [1024], P(('dp', 'tensor')), may hold values from -6 to 6
- grad_out: bfloat16 [8192, 1024], P(('dp', 'tensor')), may hold values from -6 to 6
Outputs:
- output: bfloat16 [8192, 1024], P(('dp', 'tensor'))
- grad_tokens: bfloat16 [8192, 1024], P(('dp', 'tensor'))
- grad_ln1_gain: float32 [1024], P(('dp', 'tensor'))
- grad_ln1_bias: float32 [1024], P(('dp', 'tensor'))
- grad_w_qkv: float32 [1024, 3072], P('dp', 'tensor')
- grad_b_qv: float32 [128, 16], P('tensor', 'dp')
- grad_w_out: float32 [1024, 1024], P('tensor', 'dp')
- grad_b_out: float32 [1024], P(('dp', 'tensor'))
- grad_ln2_gain: float32 [1024], P(('dp', 'tensor'))
- grad_ln2_bias: float32 [1024], P(('dp', 'tensor'))
- grad_w_up: float32 [1024, 4096], P('dp', 'tensor')
- grad_b_up: float32 [256, 16], P('tensor', 'dp')
- grad_w_down: float32 [4096, 1024], P('tensor', 'dp')
- grad_b_down: float32 [1024], P(('dp', 'tensor'))
Inputs may be any that keep to these rules, and one draw needn't show every extreme that they name: starts[s, p] lies in the p-th of 4 equal regions of the sequence, and the span of 256 tokens from it ends inside that region.
All inputs are finite; a program needn't handle non-finite values.
Results may differ from a plain program's by a relative error of at most 0.02.
Values may be sent and summed in bfloat16 or wider, within the bound.
A program may use at most 128 MiB of HBM per device.

v0:
```python
import jax
import jax.numpy as jnp
from jax import lax
from jax.sharding import PartitionSpec as P

HD = 64
PIECE = 256
QBLOCK = 512
EPS = 1e-05
ROOT = 0.7978845608028654


def gelu_tanh(values):
    return 0.5 * values * (1.0 + jnp.tanh(ROOT * (values + 0.044715 * values * values * values)))


def normalize(values):
    center = jnp.mean(values, axis=-1, keepdims=True)
    shifted = values - center
    inverse = lax.rsqrt(jnp.mean(shifted * shifted, axis=-1, keepdims=True) + EPS)
    return (shifted * inverse, inverse)


def norm_back(grad_normed, normed, inverse, gain):
    scaled = grad_normed * gain
    return inverse * (
        scaled
        - jnp.mean(scaled, axis=-1, keepdims=True)
        - normed * jnp.mean(scaled * normed, axis=-1, keepdims=True)
    )


def dot_last(left, right):
    return lax.dot_general(
        left, right, (((1,), (1,)), ((), ())), preferred_element_type=jnp.float32
    )


def dot_first(left, right):
    return lax.dot_general(
        left, right, (((0,), (0,)), ((), ())), preferred_element_type=jnp.float32
    )


def gather_rows(values):
    return lax.all_gather(values, "tensor", axis=0, tiled=True)


def gather_grads(values):
    return lax.all_gather(values, "tensor", axis=0, tiled=True)


def reduce_rows(left, weight, rows):

    def term(start, count):
        return jnp.dot(left, weight, preferred_element_type=jnp.float32)

    return lax.psum_scatter(
        term(jnp.int32(0), lax.axis_size("tensor") * rows).astype(jnp.bfloat16),
        "tensor",
        scatter_dimension=0,
        tiled=True,
    ).astype(jnp.float32)


def reduce_grads(left, weight, rows):

    def term(start, count):
        return dot_last(left, weight)

    return lax.psum_scatter(
        term(jnp.int32(0), lax.axis_size("tensor") * rows).astype(jnp.bfloat16),
        "tensor",
        scatter_dimension=0,
        tiled=True,
    ).astype(jnp.float32)


def piece_ids(start_row, length):
    places = jnp.arange(length, dtype=jnp.int32)
    inside = (places[:, None] >= start_row[None, :]) & (
        places[:, None] < start_row[None, :] + PIECE
    )
    labels = jnp.arange(1, start_row.shape[0] + 1, dtype=jnp.int32)
    return jnp.sum(jnp.where(inside, labels[None, :], 0), axis=1)


def allowed_block(row_ids, row_places, key_ids, key_places):
    causal = key_places[None, :] <= row_places[:, None]
    picture = (row_ids[:, None] == key_ids[None, :]) & (row_ids[:, None] > 0)
    return causal | picture


def block_scores(by_seq, start_rows, block_index):
    length = by_seq.shape[1]
    per_seq = length // QBLOCK
    seq_index = block_index // per_seq
    first_row = block_index % per_seq * QBLOCK
    sequence = lax.dynamic_index_in_dim(by_seq, seq_index, 0, keepdims=False)
    key_ids = piece_ids(lax.dynamic_index_in_dim(start_rows, seq_index, 0, keepdims=False), length)
    query_rows = lax.dynamic_slice_in_dim(sequence, first_row, QBLOCK, 0)[:, :, 0]
    key_rows = sequence[:, :, 1]
    value_rows = sequence[:, :, 2]
    row_ids = lax.dynamic_slice_in_dim(key_ids, first_row, QBLOCK, 0)
    row_places = first_row + jnp.arange(QBLOCK, dtype=jnp.int32)
    scores = (
        jnp.einsum("qhd,khd->hqk", query_rows, key_rows, preferred_element_type=jnp.float32) * 0.125
    )
    places = jnp.arange(length, dtype=jnp.int32)
    scores = jnp.where(allowed_block(row_ids, row_places, key_ids, places)[None], scores, -1e30)
    return (seq_index, first_row, query_rows, key_rows, value_rows, scores)


def attention_forward(by_seq, start_rows):
    total_blocks = by_seq.shape[0] * (by_seq.shape[1] // QBLOCK)

    def attend(block_index):
        _, _, query_rows, key_rows, value_rows, scores = block_scores(
            by_seq, start_rows, block_index
        )
        peak = jnp.max(scores, axis=-1, keepdims=True)
        log_total = peak + jnp.log(jnp.sum(jnp.exp(scores - peak), axis=-1, keepdims=True))
        probs = jnp.exp(scores - log_total)
        heads = jnp.einsum(
            "hqk,khd->qhd",
            probs.astype(jnp.bfloat16),
            value_rows,
            preferred_element_type=jnp.float32,
        )
        return (heads.astype(jnp.bfloat16), log_total)

    return lax.map(attend, jnp.arange(total_blocks, dtype=jnp.int32))


def attention_backward(by_seq, start_rows, log_totals, grad_heads):
    total_blocks = by_seq.shape[0] * (by_seq.shape[1] // QBLOCK)
    empty = jnp.zeros(by_seq.shape[:3] + (HD,), jnp.float32)

    def step(carry, item):
        grad_keys, grad_values = carry
        block_index, log_total = item
        seq_index, first_row, query_rows, key_rows, value_rows, scores = block_scores(
            by_seq, start_rows, block_index
        )
        grad_seq = lax.dynamic_index_in_dim(grad_heads, seq_index, 0, keepdims=False)
        grad_rows = lax.dynamic_slice_in_dim(grad_seq, first_row, QBLOCK, 0)
        probs = jnp.exp(scores - log_total)
        grad_probs = jnp.einsum(
            "qhd,khd->hqk", grad_rows, value_rows, preferred_element_type=jnp.float32
        )
        inner = jnp.sum(probs * grad_probs, axis=-1, keepdims=True)
        grad_scores = (probs * (grad_probs - inner)).astype(jnp.bfloat16)
        grad_query = (
            jnp.einsum("hqk,khd->qhd", grad_scores, key_rows, preferred_element_type=jnp.float32)
            * 0.125
        )
        key_term = (
            jnp.einsum("hqk,qhd->khd", grad_scores, query_rows, preferred_element_type=jnp.float32)
            * 0.125
        )
        value_term = jnp.einsum(
            "hqk,qhd->khd",
            probs.astype(jnp.bfloat16),
            grad_rows,
            preferred_element_type=jnp.float32,
        )
        grad_keys = lax.dynamic_update_index_in_dim(
            grad_keys,
            lax.dynamic_index_in_dim(grad_keys, seq_index, 0, keepdims=False) + key_term,
            seq_index,
            0,
        )
        grad_values = lax.dynamic_update_index_in_dim(
            grad_values,
            lax.dynamic_index_in_dim(grad_values, seq_index, 0, keepdims=False) + value_term,
            seq_index,
            0,
        )
        return ((grad_keys, grad_values), grad_query)

    (grad_keys, grad_values), grad_query = lax.scan(
        step, (empty, empty), (jnp.arange(total_blocks, dtype=jnp.int32), log_totals)
    )
    return (grad_query, grad_keys, grad_values)


def per_device(
    tokens_in,
    starts,
    ln1_gain,
    ln1_bias,
    w_qkv,
    b_qv,
    w_out,
    b_out,
    ln2_gain,
    ln2_bias,
    w_up,
    b_up,
    w_down,
    b_down,
    grad_out,
):
    rows = tokens_in.shape[0]
    gain_one, shift_one, bias_out, gain_two, shift_two, bias_down = (
        lax.all_gather(ln1_gain, ("dp", "tensor"), axis=0, tiled=True),
        lax.all_gather(ln1_bias, ("dp", "tensor"), axis=0, tiled=True),
        lax.all_gather(b_out, ("dp", "tensor"), axis=0, tiled=True),
        lax.all_gather(ln2_gain, ("dp", "tensor"), axis=0, tiled=True),
        lax.all_gather(ln2_bias, ("dp", "tensor"), axis=0, tiled=True),
        lax.all_gather(b_down, ("dp", "tensor"), axis=0, tiled=True),
    )
    weight_qkv, bias_qv, weight_out = (
        lax.all_gather(w_qkv, "dp", axis=0, tiled=True),
        lax.all_gather(b_qv, "dp", axis=1, tiled=True),
        lax.all_gather(w_out, "dp", axis=1, tiled=True),
    )
    weight_up, bias_up, weight_down = (
        lax.all_gather(w_up, "dp", axis=0, tiled=True),
        lax.all_gather(b_up, "dp", axis=1, tiled=True),
        lax.all_gather(w_down, "dp", axis=1, tiled=True),
    )
    local_heads = weight_qkv.shape[1] // (3 * HD)
    seq_count = starts.shape[0]
    inputs = tokens_in.astype(jnp.float32)
    normed_one, inverse_one = normalize(inputs)
    gathered_one = gather_rows((normed_one * gain_one + shift_one).astype(jnp.bfloat16))
    group = gathered_one.shape[0]
    length = group // seq_count
    bias_pair = bias_qv.astype(jnp.float32).reshape(local_heads, 2, HD)
    full_bias = jnp.stack(
        [bias_pair[:, 0], jnp.zeros_like(bias_pair[:, 0]), bias_pair[:, 1]], axis=1
    )
    projected = (
        jnp.dot(gathered_one, weight_qkv, preferred_element_type=jnp.float32).reshape(
            group, local_heads, 3, HD
        )
        + full_bias
    ).astype(jnp.bfloat16)
    by_seq = projected.reshape(seq_count, length, local_heads, 3, HD)
    heads_blocks, log_totals = attention_forward(by_seq, starts)
    heads_out = heads_blocks.reshape(group, local_heads * HD)
    middle = inputs + (reduce_rows(heads_out, weight_out, rows) + bias_out)
    normed_two, inverse_two = normalize(middle)
    rounded_two = (normed_two * gain_two + shift_two).astype(jnp.bfloat16)
    grad_final = grad_out.astype(jnp.float32)
    grad_bias_down = jnp.sum(grad_final, axis=0)
    gathered_two = gather_rows(rounded_two)
    up_proj = jnp.dot(gathered_two, weight_up, preferred_element_type=jnp.float32) + bias_up.astype(
        jnp.float32
    ).reshape(-1)
    hidden_act, gelu_pull = jax.vjp(gelu_tanh, up_proj)
    hidden_low = hidden_act.astype(jnp.bfloat16)
    output = (middle + reduce_rows(hidden_low, weight_down, rows) + bias_down).astype(jnp.bfloat16)
    grad_branch = gather_grads(grad_out)
    grad_w_down = dot_first(hidden_low, grad_branch)
    grad_up = gelu_pull(dot_last(grad_branch, weight_down))[0].astype(jnp.bfloat16)
    grad_b_up = jnp.sum(grad_up, axis=0, dtype=jnp.float32).reshape(bias_up.shape)
    grad_w_up = dot_first(gathered_two, grad_up)
    grad_two = reduce_grads(grad_up, weight_up, rows)
    grad_w_up, grad_b_up, grad_w_down = (
        lax.psum_scatter(
            grad_w_up.astype(jnp.bfloat16), "dp", scatter_dimension=0, tiled=True
        ).astype(jnp.float32),
        lax.psum_scatter(
            grad_b_up.astype(jnp.bfloat16), "dp", scatter_dimension=1, tiled=True
        ).astype(jnp.float32),
        lax.psum_scatter(
            grad_w_down.astype(jnp.bfloat16), "dp", scatter_dimension=1, tiled=True
        ).astype(jnp.float32),
    )
    grad_gain_two = jnp.sum(grad_two * normed_two, axis=0)
    grad_shift_two = jnp.sum(grad_two, axis=0)
    grad_middle = grad_final + norm_back(grad_two, normed_two, inverse_two, gain_two)
    grad_bias_out = jnp.sum(grad_middle, axis=0)
    grad_attn = gather_grads(grad_middle.astype(jnp.bfloat16))
    grad_w_out = dot_first(heads_out, grad_attn)
    grad_heads = (
        dot_last(grad_attn, weight_out)
        .astype(jnp.bfloat16)
        .reshape(seq_count, length, local_heads, HD)
    )
    grad_query, grad_keys, grad_values = attention_backward(by_seq, starts, log_totals, grad_heads)
    grad_proj = jnp.stack(
        [
            grad_query.reshape(group, local_heads, HD),
            grad_keys.reshape(group, local_heads, HD),
            grad_values.reshape(group, local_heads, HD),
        ],
        axis=2,
    ).astype(jnp.bfloat16)
    grad_b_qv = jnp.sum(grad_proj[:, :, 0::2], axis=0, dtype=jnp.float32).reshape(bias_qv.shape)
    grad_flat = grad_proj.reshape(group, 3 * local_heads * HD)
    grad_w_qkv = dot_first(gathered_one, grad_flat)
    grad_one = reduce_grads(grad_flat, weight_qkv, rows)
    grad_w_qkv, grad_b_qv, grad_w_out = (
        lax.psum_scatter(
            grad_w_qkv.astype(jnp.bfloat16), "dp", scatter_dimension=0, tiled=True
        ).astype(jnp.float32),
        lax.psum_scatter(
            grad_b_qv.astype(jnp.bfloat16), "dp", scatter_dimension=1, tiled=True
        ).astype(jnp.float32),
        lax.psum_scatter(
            grad_w_out.astype(jnp.bfloat16), "dp", scatter_dimension=1, tiled=True
        ).astype(jnp.float32),
    )
    grad_gain_one = jnp.sum(grad_one * normed_one, axis=0)
    grad_shift_one = jnp.sum(grad_one, axis=0)
    grad_tokens = (grad_middle + norm_back(grad_one, normed_one, inverse_one, gain_one)).astype(
        jnp.bfloat16
    )
    summed = (
        lax.psum_scatter(grad_gain_one, ("dp", "tensor"), scatter_dimension=0, tiled=True),
        lax.psum_scatter(grad_shift_one, ("dp", "tensor"), scatter_dimension=0, tiled=True),
        lax.psum_scatter(grad_bias_out, ("dp", "tensor"), scatter_dimension=0, tiled=True),
        lax.psum_scatter(grad_gain_two, ("dp", "tensor"), scatter_dimension=0, tiled=True),
        lax.psum_scatter(grad_shift_two, ("dp", "tensor"), scatter_dimension=0, tiled=True),
        lax.psum_scatter(grad_bias_down, ("dp", "tensor"), scatter_dimension=0, tiled=True),
    )
    return (
        output,
        grad_tokens,
        summed[0],
        summed[1],
        grad_w_qkv,
        grad_b_qv,
        grad_w_out,
        summed[2],
        summed[3],
        summed[4],
        grad_w_up,
        grad_b_up,
        grad_w_down,
        summed[5],
    )


def solution(mesh):
    return jax.shard_map(
        per_device,
        mesh=mesh,
        in_specs=(
            P(("dp", "tensor"), None),
            P("dp", None),
            P(("dp", "tensor")),
            P(("dp", "tensor")),
            P("dp", "tensor"),
            P("tensor", "dp"),
            P("tensor", "dp"),
            P(("dp", "tensor")),
            P(("dp", "tensor")),
            P(("dp", "tensor")),
            P("dp", "tensor"),
            P("tensor", "dp"),
            P("tensor", "dp"),
            P(("dp", "tensor")),
            P(("dp", "tensor"), None),
        ),
        out_specs=(
            P(("dp", "tensor"), None),
            P(("dp", "tensor"), None),
            P(("dp", "tensor")),
            P(("dp", "tensor")),
            P("dp", "tensor"),
            P("tensor", "dp"),
            P("tensor", "dp"),
            P(("dp", "tensor")),
            P(("dp", "tensor")),
            P(("dp", "tensor")),
            P("dp", "tensor"),
            P("tensor", "dp"),
            P("tensor", "dp"),
            P(("dp", "tensor")),
        ),
        check_vma=False,
    )
```

profile of v0, /device:TPU:12, one launch (start us, length us, event | category | flops | bytes accessed | tf_op | source)
XLA Modules:
  0.0 705.2 jit_solution(5103127675943364345)
XLA Ops:
  12.2 41.6 %all-reduce.15 = (f32[1024]{0:T(1024)S(1)}, f32[1024]{0:T(1024)S(1)}, f32[1024]{0:T(1024)S(1)}, f32[1024]{0:T(1024)S(1)}, f32[1024]{0:T(1024)S(1)}) all-reduce(f32[1024]{0:T(1024)S(1)} %dynamic-update-slice.4, f32[1024]{0:T(1024)S(1)} %dynamic-update-slice.3, ...), channel_id=1, replica_groups=mesh['dp'=8,'tensor'=4] {'dp','tensor'}, use_global_device_ids=true, to_apply=%add.4 | all-reduce | flops 5120 | bytes 40960
  58.5 7.9 %all-gather = bf16[8,2,32]{2,1,0:T(2,128)(2,1)S(1)} all-gather(bf16[1,2,32]{2,1,0:T(2,128)(2,1)} %bitcast.220), channel_id=1, replica_groups=mesh['dp'=8,'tensor'=4] {'dp'}, dimensions={0}, use_global_device_ids=true | all-gather | bytes 1152 | tf_op jit(solution)/shard_map/all_gather | solution.py:215
  66.7 10.4 %all_gather.53 = bf16[256,1024]{1,0:T(8,128)(2,1)S(1)} all-gather(bf16[256,128]{1,0:T(8,128)(2,1)} %param.25), channel_id=1, replica_groups=mesh['dp'=8,'tensor'=4] {'dp'}, dimensions={1}, use_global_device_ids=true | all-gather | bytes 589824 | tf_op jit(solution)/shard_map/all_gather | solution.py:216
  77.1 24.8 %all-gather.10.cloned.1.call-done = bf16[1024,1024]{1,0:T(8,128)(2,1)} async-done(((bf16[256,1024]{1,0:T(8,128)(2,1)}), bf16[1024,1024]{1,0:T(8,128)(2,1)}) %all-gather.10.cloned.1.call-update) | async-done | bytes 2097168 | tf_op jit(solution)/shard_map/all_gather | solution.py:46
  106.5 19.6 %while.30 = (s32[]{:T(128)}, bf16[2,512,4,64]{1,3,2,0:T(8,128)(2,1)S(1)}, f32[2,4,512,1]{2,1,3,0:T(4,128)S(1)}, s32[2]{0:T(128)S(1)}, s32[1,4]{1,0:T(1,128)S(1)}...) while((s32[]{:T(128)}, ...), condition=%wide.region_6.7_spmd, body=%wide.region_2.6_spmd.sunk | while | flops 562186240 | bytes 30494096 | solution.py:132
  130.4 42.5 %reduce-scatter.15.cloned.1.call-done = bf16[256,1024]{1,0:T(8,128)(2,1)} async-done(((bf16[1024,1024]{1,0:T(8,128)(2,1)}), bf16[256,1024]{1,0:T(8,128)(2,1)}) %reduce-scatter.15.cloned.1.call-update) | async-done | bytes 524304 | tf_op jit(solution)/shard_map/reduce_scatter | solution.py:58
  179.1 9.0 %all-gather.1 = bf16[8,2,64]{2,1,0:T(2,128)(2,1)S(1)} all-gather(bf16[1,2,64]{2,1,0:T(2,128)(2,1)S(1)} %bitcast.221), channel_id=1, replica_groups=mesh['dp'=8,'tensor'=4] {'dp'}, dimensions={0}, use_global_device_ids=true | all-gather | bytes 2304 | tf_op jit(solution)/shard_map/all_gather | solution.py:220
  188.2 14.1 %all-gather.16.cloned.1.call-done = bf16[1024,1024]{1,0:T(8,128)(2,1)} async-done(((bf16[128,1024]{1,0:T(8,128)(2,1)}), bf16[1024,1024]{1,0:T(8,128)(2,1)}) %all-gather.16.cloned.1.call-update) | async-done | bytes 2097168 | tf_op jit(solution)/shard_map/all_gather | solution.py:219
  202.4 46.4 %all-gather.14.cloned.1.call-done = bf16[1024,1024]{1,0:T(8,128)(2,1)} async-done(((bf16[256,1024]{1,0:T(8,128)(2,1)}), bf16[1024,1024]{1,0:T(8,128)(2,1)}) %all-gather.14.cloned.1.call-update) | async-done | bytes 2097168 | tf_op jit(solution)/shard_map/all_gather | solution.py:46
  255.3 39.4 %all-gather.20.cloned.1.call-done = bf16[1024,1024]{1,0:T(8,128)(2,1)} async-done(((bf16[256,1024]{1,0:T(8,128)(2,1)}), bf16[1024,1024]{1,0:T(8,128)(2,1)}) %all-gather.20.cloned.1.call-update) | async-done | bytes 2097168 | tf_op jit(solution)/shard_map/all_gather | solution.py:50
  294.7 29.8 %all-gather.18.cloned.1.call-done = bf16[1024,1024]{1,0:T(8,128)(2,1)} async-done(((bf16[1024,128]{1,0:T(8,128)(2,1)}), bf16[1024,1024]{1,0:T(8,128)(2,1)}) %all-gather.18.cloned.1.call-update) | async-done | bytes 2097168 | tf_op jit(solution)/shard_map/all_gather | solution.py:221
  324.5 9.6 %fusion.71 = (bf16[1024]{0:T(1024)(128)(2,1)}, bf16[1024,1024]{1,0:T(8,128)(2,1)S(1)}) fusion(f32[1024,1024]{1,0:T(8,128)} %fusion.76, f32[1024]{0:T(1024)S(1)} %reshape.318, bf16[1024,1024]{1,0:T(8,128)(2,1)} %all-gather.20.cloned.1.call-done, bf16[1024,1024]{1,0:T(8,128)(2,1)} %all-gather.18.cloned.1.call-done), kind=kOutput, calls=%fused_computation.142 | convolution fusion | flops 2174745600 | bytes 10491904 | tf_op jit(solution)/shard_map/dot_general | solution.py:34
  339.2 43.2 %reduce-scatter.19.cloned.1.call-done = bf16[256,1024]{1,0:T(8,128)(2,1)} async-done(((bf16[1024,1024]{1,0:T(8,128)(2,1)}), bf16[256,1024]{1,0:T(8,128)(2,1)}) %reduce-scatter.19.cloned.1.call-update) | async-done | bytes 524304 | tf_op jit(solution)/shard_map/reduce_scatter | solution.py:71
  387.9 7.2 %convolution_convert_fusion = bf16[1024,1024]{1,0:T(8,128)(2,1)} fusion(bf16[1024,1024]{1,0:T(8,128)(2,1)} %all-gather.20.cloned.1.call-done, f32[1024,1024]{1,0:T(8,128)} %fusion.76, f32[1024]{0:T(1024)S(1)} %reshape.318), kind=kOutput, calls=%fused_computation.82 | convolution fusion | flops 2159017984 | bytes 8392704 | tf_op jit(solution)/shard_map/dot_general | solution.py:40
  405.3 26.9 %all-gather.22.cloned.1.call-done = bf16[1024,1024]{1,0:T(8,128)(2,1)} async-done(((bf16[256,1024]{1,0:T(8,128)(2,1)}), bf16[1024,1024]{1,0:T(8,128)(2,1)}) %all-gather.22.cloned.1.call-update) | async-done | bytes 2097168 | tf_op jit(solution)/shard_map/all_gather | solution.py:50
  442.2 56.8 %while.31 = (s32[]{:T(128)}, f32[1,1024,4,64]{1,3,2,0:T(8,128)S(1)}, f32[1,1024,4,64]{1,3,2,0:T(8,128)}, bf16[2,512,4,64]{1,0,3,2:T(2,128)(2,1)}, s32[2]{0:T(128...) while((s32[]{:T(128)}, ...), condition=%wide.region_17.18_spmd, body=%wide.region_14.17_spmd.sunk | while | flops 1376798720 | bytes 76885448 | solution.py:181
  460.6 9.9 %dynamic_update_slice.31 = bf16[2,512,4,64]{1,0,3,2:T(2,128)(2,1)} dynamic-update-slice(bf16[2,512,4,64]{1,0,3,2:T(2,128)(2,1)} %get-tuple-element.503, bf16[1,512,4,64]{1,0,3,2:T(2,128)(2,1)} %copy.86, s32[]{:T(128)S(6)} %copy.108, s32[]{:T(128)} %constant.208.clone.1..sunk.1, s32[]{:T(128)} %constant.208.clone.1..sunk.1, s32[]{:T(128)} %constant.208.clone.1..sunk.1) | dynamic-update-slice | bytes 524292 | tf_op jit(solution)/shard_map/while/body/jit(dynamic_update_index_in_dim)/dynamic_update_slice | solution.py:181
  488.9 9.9 %dynamic_update_slice.31 = bf16[2,512,4,64]{1,0,3,2:T(2,128)(2,1)} dynamic-update-slice(bf16[2,512,4,64]{1,0,3,2:T(2,128)(2,1)} %get-tuple-element.503, bf16[1,512,4,64]{1,0,3,2:T(2,128)(2,1)} %copy.86, s32[]{:T(128)S(6)} %copy.108, s32[]{:T(128)} %constant.208.clone.1..sunk.1, s32[]{:T(128)} %constant.208.clone.1..sunk.1, s32[]{:T(128)} %constant.208.clone.1..sunk.1) | dynamic-update-slice | bytes 524292 | tf_op jit(solution)/shard_map/while/body/jit(dynamic_update_index_in_dim)/dynamic_update_slice | solution.py:181
  512.8 7.1 %convolution_convert_fusion.3 = bf16[1024,1024]{1,0:T(8,128)(2,1)} fusion(bf16[1024,1024]{1,0:T(8,128)(2,1)} %all-gather.18.cloned.1.call-done, f32[1024,1024]{1,0:T(8,128)} %fusion.76, f32[1024]{0:T(1024)S(1)} %reshape.318), kind=kOutput, calls=%fused_computation.85 | convolution fusion | flops 2159017984 | bytes 8392704 | tf_op jit(solution)/shard_map/dot_general | solution.py:56
  526.8 22.9 %all-reduce.16 = (bf16[32,16]{1,0:T(8,128)(2,1)S(1)}, bf16[64,16]{1,0:T(8,128)(2,1)S(1)}) all-reduce(bf16[32,16]{1,0:T(8,128)(2,1)S(1)} %convert_element_type.163, bf16[64,16]{1,0:T(8,128)(2,1)S(1)} %convert_element_type.169), channel_id=9, replica_groups=mesh['dp'=8,'tensor'=4] {'dp'}, use_global_device_ids=true, to_apply=%region_27.28.clone | all-reduce | flops 1536 | bytes 6144
  551.2 7.5 %reduce-scatter.27.cloned.1.call-done = bf16[128,256]{1,0:T(8,128)(2,1)} async-done(((bf16[1024,256]{1,0:T(8,128)(2,1)}), bf16[128,256]{1,0:T(8,128)(2,1)}) %reduce-scatter.27.cloned.1.call-update) | async-done | bytes 65552
  560.3 40.0 %reduce-scatter.23.cloned.1.call-done = bf16[128,768]{1,0:T(8,128)(2,1)} async-done(((bf16[1024,768]{1,0:T(8,128)(2,1)}), bf16[128,768]{1,0:T(8,128)(2,1)}) %reduce-scatter.23.cloned.1.call-update) | async-done | bytes 196624 | tf_op jit(solution)/shard_map/reduce_scatter | solution.py:297
  602.1 43.3 %reduce-scatter.21.cloned.1.call-done = bf16[256,1024]{1,0:T(8,128)(2,1)} async-done(((bf16[1024,1024]{1,0:T(8,128)(2,1)}), bf16[256,1024]{1,0:T(8,128)(2,1)}) %reduce-scatter.21.cloned.1.call-update) | async-done | bytes 524304 | tf_op jit(solution)/shard_map/reduce_scatter | solution.py:71
  647.0 45.3 %all-reduce.14 = (f32[1024]{0:T(1024)S(1)}, f32[1024]{0:T(1024)S(1)}, f32[1024]{0:T(1024)S(1)}, f32[1024]{0:T(1024)S(1)}, f32[1024]{0:T(1024)S(1)}, /*index=5*/f32[1024]{0:T(1024)S(1)}, f32[1024]{0:T(1024)S(1)}) all-reduce(f32[1024]{0:T(1024)S(1)} %dynamic-update-slice.5, ...), channel_id=1, replica_groups=mesh['dp'=8,'tensor'=4] {'dp','tensor'}, use_global_device_ids=true, to_apply=%add.5 | all-reduce | flops 7168 | bytes 57344
  (225 shorter events, 143.1 us)
Async XLA Ops:
  7.2 70.0 %all-gather.12.cloned.1.call-start = ((), (), s32[]{:S(2)}) async-start(), calls=%async_computation.9 | async-start | bytes 1769472 | tf_op jit(solution)/shard_map/all_gather | solution.py:214
  7.9 94.0 %all-gather.10.cloned.1.call-start = ((), (), s32[]{:S(2)}) async-start(), calls=%async_computation.8 | async-start | bytes 2621440 | tf_op jit(solution)/shard_map/all_gather | solution.py:46
  58.5 114.4 %reduce-scatter.15.cloned.1.call-start = ((), (), s32[]{:S(2)}) async-start(), calls=%async_computation.10 | async-start | bytes 2621440 | tf_op jit(solution)/shard_map/reduce_scatter | solution.py:58
  77.1 49.6 %copy-start.8 = (bf16[256,1024]{1,0:T(8,128)(2,1)}, bf16[256,1024]{1,0:T(8,128)(2,1)S(1)}, u32[]{:S(2)}) copy-start(bf16[256,1024]{1,0:T(8,128)(2,1)S(1)} %all_gather.53) | copy-start | bytes 1572868
  129.7 49.4 %copy-start.21 = (bf16[64,2]{0,1:T(2,128)(2,1)S(1)}, bf16[64,2]{0,1:T(2,128)(2,1)}, u32[]{:S(2)}) copy-start(bf16[64,2]{0,1:T(2,128)(2,1)} %param.30) | copy-start | bytes 772
  129.7 72.6 %all-gather.16.cloned.1.call-start = ((), (), s32[]{:S(2)}) async-start(), calls=%async_computation.12 | async-start | bytes 2359296 | tf_op jit(solution)/shard_map/all_gather | solution.py:219
  130.3 118.5 %all-gather.14.cloned.1.call-start = ((), (), s32[]{:S(2)}) async-start(), calls=%async_computation.11 | async-start | bytes 2621440 | tf_op jit(solution)/shard_map/all_gather | solution.py:46
  177.7 117.0 %all-gather.20.cloned.1.call-start = ((), (), s32[]{:S(2)}) async-start(), calls=%async_computation.15 | async-start | bytes 2621440 | tf_op jit(solution)/shard_map/all_gather | solution.py:50
  178.3 146.2 %all-gather.18.cloned.1.call-start = ((), (), s32[]{:S(2)}) async-start(), calls=%async_computation.13 | async-start | bytes 2359296 | tf_op jit(solution)/shard_map/all_gather | solution.py:221
  179.0 203.4 %reduce-scatter.19.cloned.1.call-start = ((), (), s32[]{:S(2)}) async-start(), calls=%async_computation.16 | async-start | bytes 2621440 | tf_op jit(solution)/shard_map/reduce_scatter | solution.py:71
  335.4 47.0 %copy-start.1 = (bf16[256,1024]{1,0:T(8,128)(2,1)S(1)}, bf16[256,1024]{1,0:T(8,128)(2,1)}, u32[]{:S(2)}) copy-start(bf16[256,1024]{1,0:T(8,128)(2,1)} %reduce-scatter.15.cloned.1.call-done) | copy-start | bytes 1572868
  335.4 48.7 %copy-start.7 = (bf16[256,1024]{1,0:T(8,128)(2,1)S(1)}, bf16[256,1024]{1,0:T(8,128)(2,1)}, u32[]{:S(2)}) copy-start(bf16[256,1024]{1,0:T(8,128)(2,1)} %param.33) | copy-start | bytes 1572868
  339.1 93.1 %all-gather.22.cloned.1.call-start = ((), (), s32[]{:S(2)}) async-start(), calls=%async_computation.17 | async-start | bytes 2621440 | tf_op jit(solution)/shard_map/all_gather | solution.py:50
  387.7 133.9 %reduce-scatter.29.cloned.1.call-start = ((), (), s32[]{:S(2)}) async-start(), calls=%async_computation.22 | async-start | bytes 2359296
  399.2 124.3 %reduce-scatter.25.cloned.1.call-start = ((), (), s32[]{:S(2)}) async-start(), calls=%async_computation.20 | async-start | bytes 2359296 | tf_op jit(solution)/shard_map/reduce_scatter | solution.py:262
  405.3 153.4 %reduce-scatter.27.cloned.1.call-start = ((), (), s32[]{:S(2)}) async-start(), calls=%async_computation.21 | async-start | bytes 589824
  437.4 163.0 %reduce-scatter.23.cloned.1.call-start = ((), (), s32[]{:S(2)}) async-start(), calls=%async_computation.19 | async-start | bytes 1769472 | tf_op jit(solution)/shard_map/reduce_scatter | solution.py:297
  507.6 137.8 %reduce-scatter.21.cloned.1.call-start = ((), (), s32[]{:S(2)}) async-start(), calls=%async_computation.18 | async-start | bytes 2621440 | tf_op jit(solution)/shard_map/reduce_scatter | solution.py:71
  512.8 183.0 %reduce-scatter.17.cloned.1.call-start = ((), (), s32[]{:S(2)}) async-start(), calls=%async_computation.14 | async-start | bytes 2621440 | tf_op jit(solution)/shard_map/reduce_scatter | solution.py:58
  519.9 125.5 %copy-start.15 = (f32[1024]{0:T(1024)S(1)}, f32[1024]{0:T(1024)}, u32[]{:S(2)}) copy-start(f32[1024]{0:T(1024)} %copy-done.14) | copy-start | bytes 12292
  519.9 125.5 %copy-start.17 = (f32[256]{0:T(256)S(1)}, f32[256]{0:T(256)}, u32[]{:S(2)}) copy-start(f32[256]{0:T(256)} %copy-done.16) | copy-start | bytes 3076
  519.9 125.5 %copy-start.19 = (f32[256]{0:T(256)S(1)}, f32[256]{0:T(256)}, u32[]{:S(2)}) copy-start(f32[256]{0:T(256)} %copy-done.18) | copy-start | bytes 3076
  519.9 175.9 %copy-start.2 = (bf16[256,1024]{1,0:T(8,128)(2,1)S(1)}, bf16[256,1024]{1,0:T(8,128)(2,1)}, u32[]{:S(2)}) copy-start(bf16[256,1024]{1,0:T(8,128)(2,1)} %reduce-scatter.15.cloned.1.call-done) | copy-start | bytes 1572868
  519.9 175.9 %copy-start.5 = (f32[256,1024]{1,0:T(8,128)S(1)}, f32[256,1024]{1,0:T(8,128)}, u32[]{:S(2)}) copy-start(f32[256,1024]{1,0:T(8,128)} %copy-done.4) | copy-start | bytes 3145732
  (19 other events, 173.5 us)
Sparse Core Ops, SparseCore 0:
  9.9 26.7 all-gather.11
  58.5 43.3 all-gather.9
  129.8 42.9 reduce-scatter.14
  174.6 27.7 all-gather.15
  204.3 44.4 all-gather.13
  250.2 44.4 all-gather.19
  296.6 27.8 all-gather.17
  339.2 43.1 reduce-scatter.18
  387.8 44.3 all-gather.21
  435.3 41.1 reduce-scatter.28
  479.9 41.1 reduce-scatter.24
  524.5 34.1 reduce-scatter.26
  562.0 38.3 reduce-scatter.22
  602.5 42.8 reduce-scatter.20
  647.5 43.8 reduce-scatter.16
where the time goes:
time: 711 us; the launch traced here: 705 us
  waiting for transfers between devices  361 us (51%)
  blocking collectives  137 us (19%)
  matrix products  91 us (13%)
  local copies, waits for them, and re-layouts  52.4 us (7%)
  other arithmetic  39.5 us (6%)
  between operations  15.2 us (2%)
  loops' own time  8.27 us (1%)
    unnamed x3, blocking collectives  110 us
    reduce_scatter x2, waiting for transfers between devices, reduce_grads(): lax.psum_scatter(term(jnp.int32(0), lax.axis_size('tensor') * rows).astyp...  86.5 us
    all_gather x2, waiting for transfers between devices, gather_rows(): return lax.all_gather(values, 'tensor', axis=0, tiled=True)  71.2 us
    all_gather x2, waiting for transfers between devices, gather_grads(): return lax.all_gather(values, 'tensor', axis=0, tiled=True)  66.2 us
    reduce_scatter x2, waiting for transfers between devices, reduce_rows(): lax.psum_scatter(term(jnp.int32(0), lax.axis_size('tensor') * rows).astyp...  42.5 us
    reduce_scatter x1, waiting for transfers between devices, per_device(): lax.psum_scatter(grad_w_qkv.astype(jnp.bfloat16), 'dp', scatter_dimension...  40 us
    all_gather x1, waiting for transfers between devices, per_device(): lax.all_gather(w_down, 'dp', axis=1, tiled=True)  29.8 us
    unnamed x78, local copies, waits for them, and re-layouts  22.9 us
  transfers between devices with their start and end apart: 15, of which 11 were waited for; matrix products, arithmetic and copies ran while one was open for 19% of the time, Pallas kernels for 0%

commit v1 on v0

--- a/solution.py
+++ b/solution.py
@@ -8,6 +8,28 @@
 QBLOCK = 512
 EPS = 1e-05
 ROOT = 0.7978845608028654
+
+
+def joined_along(blocks, dim):
+    shape = list(blocks.shape[1:])
+    shape[dim] *= blocks.shape[0]
+    return jnp.moveaxis(blocks, 0, dim).reshape(shape)
+
+
+def ring_gather(value, axis, dim):
+    devices = lax.axis_size(axis)
+    pairs = [(i, (i + 1) % devices) for i in range(devices)]
+    back = [(b, a) for a, b in pairs]
+    lower, upper = ([], [])
+    for step in range(devices - 1):
+        if step % 2 == 0:
+            lower.append(lax.ppermute(lower[-1] if lower else value, axis, pairs))
+        else:
+            upper.append(lax.ppermute(upper[-1] if upper else value, axis, back))
+    blocks = jnp.stack([*lower[::-1], value, *upper])
+    shift = lax.axis_index(axis) - len(lower)
+    blocks = blocks[(jnp.arange(devices) - shift) % devices]
+    return joined_along(blocks, dim)
 
 
 def gelu_tanh(values):
@@ -47,7 +69,7 @@
 
 
 def gather_grads(values):
-    return lax.all_gather(values, "tensor", axis=0, tiled=True)
+    return ring_gather(values, "tensor", 0)
 
 
 def reduce_rows(left, weight, rows):

time: 711 us -> 616 us (0.87)
  waiting for transfers between devices: 361 us -> 242 us
  starting transfers between devices: 1.22 us -> 11.5 us
  local copies, waits for them, and re-layouts: 52.4 us -> 59.6 us
    all_gather x2 -> x0, waiting for transfers between devices: 66.2 us -> none  [gather_grads(): return lax.all_gather(values, 'tensor', axis=0, tiled=True)]
    ppermute x0 -> x6, waiting for transfers between devices: none -> 52.3 us  [the longest x4 52.3 us: ring_gather(): lower.append(lax.ppermute(lower[-1] if lower else value, axis, pairs))]
    reduce_scatter x1, waiting for transfers between devices: 40 us -> 1.19 us  [per_device(): lax.psum_scatter(grad_w_qkv.astype(jnp.bfloat16), 'dp', scatter_dimension...]
    all_gather x2, waiting for transfers between devices: 71.2 us -> 51.3 us  [gather_rows(): return lax.all_gather(values, 'tensor', axis=0, tiled=True)]
    reduce_scatter x2, waiting for transfers between devices: 86.5 us -> 69.1 us  [reduce_grads(): lax.psum_scatter(term(jnp.int32(0), lax.axis_size('tensor') * rows).astyp...]
    all_gather x1, waiting for transfers between devices: 14.1 us -> 0.01 us  [per_device(): lax.all_gather(w_up, 'dp', axis=0, tiled=True)]
    ppermute x0 -> x6, starting transfers between devices: none -> 10.3 us  [the longest x4 9.33 us: ring_gather(): lower.append(lax.ppermute(lower[-1] if lower else value, axis, pairs))]
    unnamed x17 -> x15, waiting for transfers between devices: 10.2 us -> 1.9 us
  transfers between devices with their start and end apart: 15 -> 19, of which waited for: 11 -> 11; matrix products, arithmetic and copies ran while one was open for 19% -> 25% of each run, Pallas kernels for 0% -> 0%
where the time goes in v1:
time: 616 us; the launch traced here: 609 us
  waiting for transfers between devices  242 us (39%)
  blocking collectives  135 us (22%)
  matrix products  90.9 us (15%)
  local copies, waits for them, and re-layouts  59.6 us (10%)
  other arithmetic  46.2 us (8%)
  between operations  15.2 us (2%)
  starting transfers between devices  11.5 us (2%)
  loops' own time  8.27 us (1%)
    unnamed x3, blocking collectives  108 us
    reduce_scatter x2, waiting for transfers between devices, reduce_grads(): lax.psum_scatter(term(jnp.int32(0), lax.axis_size('tensor') * rows).astyp...  69.1 us
    ppermute x4, waiting for transfers between devices, ring_gather(): lower.append(lax.ppermute(lower[-1] if lower else value, axis, pairs))  52.3 us
    all_gather x2, waiting for transfers between devices, gather_rows(): return lax.all_gather(values, 'tensor', axis=0, tiled=True)  51.3 us
    reduce_scatter x2, waiting for transfers between devices, reduce_rows(): lax.psum_scatter(term(jnp.int32(0), lax.axis_size('tensor') * rows).astyp...  42.5 us
    all_gather x1, waiting for transfers between devices, per_device(): lax.all_gather(w_down, 'dp', axis=1, tiled=True)  23.6 us
    unnamed x74, local copies, waits for them, and re-layouts  22.9 us
    dynamic_update_slice x4, local copies, waits for them, and re-layouts, attention_backward(): lax.scan(step, (empty, empty), (jnp.arange(total_blocks, dtype=jnp.int32)...  22.2 us
  transfers between devices with their start and end apart: 19, of which 11 were waited for; matrix products, arithmetic and copies ran while one was open for 25% of the time, Pallas kernels for 0%

profile of v1, /device:TPU:12, one launch (start us, length us, event | category | flops | bytes accessed | tf_op | source)
XLA Modules:
  0.0 608.6 jit_solution(5609862049060437253)
XLA Ops:
  12.2 41.6 %all-reduce.15 = (f32[1024]{0:T(1024)S(1)}, f32[1024]{0:T(1024)S(1)}, f32[1024]{0:T(1024)S(1)}, f32[1024]{0:T(1024)S(1)}, f32[1024]{0:T(1024)S(1)}) all-reduce(f32[1024]{0:T(1024)S(1)} %dynamic-update-slice.4, f32[1024]{0:T(1024)S(1)} %dynamic-update-slice.3, ...), channel_id=1, replica_groups=mesh['dp'=8,'tensor'=4] {'dp','tensor'}, use_global_device_ids=true, to_apply=%add.4 | all-reduce | flops 5120 | bytes 40960
  58.5 7.9 %all-gather = bf16[8,2,32]{2,1,0:T(2,128)(2,1)S(1)} all-gather(bf16[1,2,32]{2,1,0:T(2,128)(2,1)} %bitcast.238), channel_id=1, replica_groups=mesh['dp'=8,'tensor'=4] {'dp'}, dimensions={0}, use_global_device_ids=true | all-gather | bytes 1152 | tf_op jit(solution)/shard_map/all_gather | solution.py:237
  66.7 10.4 %all_gather.47 = bf16[256,1024]{1,0:T(8,128)(2,1)S(1)} all-gather(bf16[256,128]{1,0:T(8,128)(2,1)} %param.25), channel_id=1, replica_groups=mesh['dp'=8,'tensor'=4] {'dp'}, dimensions={1}, use_global_device_ids=true | all-gather | bytes 589824 | tf_op jit(solution)/shard_map/all_gather | solution.py:238
  77.1 24.8 %all-gather.8.cloned.1.call-done = bf16[1024,1024]{1,0:T(8,128)(2,1)} async-done(((bf16[256,1024]{1,0:T(8,128)(2,1)}), bf16[1024,1024]{1,0:T(8,128)(2,1)}) %all-gather.8.cloned.1.call-update) | async-done | bytes 2097168 | tf_op jit(solution)/shard_map/all_gather | solution.py:68
  106.5 19.6 %while.30 = (s32[]{:T(128)}, bf16[2,512,4,64]{1,3,2,0:T(8,128)(2,1)S(1)}, f32[2,4,512,1]{2,1,3,0:T(4,128)S(1)}, s32[2]{0:T(128)S(1)}, s32[1,4]{1,0:T(1,128)S(1)}...) while((s32[]{:T(128)}, ...), condition=%wide.region_6.7_spmd, body=%wide.region_2.6_spmd.sunk | while | flops 562186240 | bytes 30494096 | solution.py:154
  130.3 42.5 %reduce-scatter.15.cloned.1.call-done = bf16[256,1024]{1,0:T(8,128)(2,1)} async-done(((bf16[1024,1024]{1,0:T(8,128)(2,1)}), bf16[256,1024]{1,0:T(8,128)(2,1)}) %reduce-scatter.15.cloned.1.call-update) | async-done | bytes 524304 | tf_op jit(solution)/shard_map/reduce_scatter | solution.py:80
  180.3 21.5 %collective-permute-done = bf16[256,1024]{1,0:T(8,128)(2,1)} collective-permute-done((bf16[256,1024]{1,0:T(8,128)(2,1)S(1)}, bf16[256,1024]{1,0:T(8,128)(2,1)}, u32[]{:S(2)}, u32[]{:S(2)}) %collective-permute-start) | collective-permute-done | bytes 524320 | tf_op jit(solution)/shard_map/ppermute | solution.py:26
  204.9 8.9 %all-gather.1 = bf16[8,2,64]{2,1,0:T(2,128)(2,1)S(1)} all-gather(bf16[1,2,64]{2,1,0:T(2,128)(2,1)S(1)} %bitcast.239), channel_id=1, replica_groups=mesh['dp'=8,'tensor'=4] {'dp'}, dimensions={0}, use_global_device_ids=true | all-gather | bytes 2304 | tf_op jit(solution)/shard_map/all_gather | solution.py:242
  222.3 26.5 %all-gather.12.cloned.1.call-done = bf16[1024,1024]{1,0:T(8,128)(2,1)} async-done(((bf16[256,1024]{1,0:T(8,128)(2,1)}), bf16[1024,1024]{1,0:T(8,128)(2,1)}) %all-gather.12.cloned.1.call-update) | async-done | bytes 2097168 | tf_op jit(solution)/shard_map/all_gather | solution.py:68
  248.8 6.5 %fusion.78 = f32[1024,1024]{1,0:T(8,128)} fusion(bf16[1024,1024]{1,0:T(8,128)(2,1)} %all-gather.12.cloned.1.call-done, bf16[1024,1024]{1,0:T(8,128)(2,1)} %all-gather.14.cloned.1.call-done), kind=kOutput, calls=%fused_computation.157 | convolution fusion | flops 2147483648 | bytes 8388608 | tf_op jit(solution)/shard_map/dot_general | solution.py:271
  255.2 23.6 %all-gather.16.cloned.1.call-done = bf16[1024,1024]{1,0:T(8,128)(2,1)} async-done(((bf16[1024,128]{1,0:T(8,128)(2,1)}), bf16[1024,1024]{1,0:T(8,128)(2,1)}) %all-gather.16.cloned.1.call-update) | async-done | bytes 2097168 | tf_op jit(solution)/shard_map/all_gather | solution.py:243
  278.9 9.6 %fusion.73 = (bf16[1024]{0:T(1024)(128)(2,1)}, bf16[1024,1024]{1,0:T(8,128)(2,1)S(1)}) fusion(f32[1024,1024]{1,0:T(8,128)} %fusion.78, f32[1024]{0:T(1024)S(1)} %reshape.375, bf16[1024,1024]{1,0:T(8,128)(2,1)} %bitcast.219, bf16[1024,1024]{1,0:T(8,128)(2,1)} %all-gather.16.cloned.1.call-done), kind=kOutput, calls=%fused_computation.153 | convolution fusion | flops 2174745600 | bytes 10491904 | tf_op jit(solution)/shard_map/dot_general | solution.py:56
  293.8 7.2 %convolution_convert_fusion = bf16[1024,1024]{1,0:T(8,128)(2,1)} fusion(bf16[1024,1024]{1,0:T(8,128)(2,1)} %bitcast.220, f32[1024,1024]{1,0:T(8,128)} %fusion.78, f32[1024]{0:T(1024)S(1)} %reshape.375), kind=kOutput, calls=%fused_computation.86 | convolution fusion | flops 2159017984 | bytes 8392704 | tf_op jit(solution)/shard_map/dot_general | solution.py:62
  305.0 6.0 convolution_convert_fusion.1
  311.1 25.7 %reduce-scatter.19.cloned.1.call-done = bf16[256,1024]{1,0:T(8,128)(2,1)} async-done(((bf16[1024,1024]{1,0:T(8,128)(2,1)}), bf16[256,1024]{1,0:T(8,128)(2,1)}) %reduce-scatter.19.cloned.1.call-update) | async-done | bytes 524304 | tf_op jit(solution)/shard_map/reduce_scatter | solution.py:93
  343.6 21.6 %collective-permute-done.3 = bf16[256,1024]{1,0:T(8,128)(2,1)} collective-permute-done((bf16[256,1024]{1,0:T(8,128)(2,1)S(1)}, bf16[256,1024]{1,0:T(8,128)(2,1)}, u32[]{:S(2)}, u32[]{:S(2)}) %collective-permute-start.3) | collective-permute-done | bytes 524320 | tf_op jit(solution)/shard_map/ppermute | solution.py:26
  369.6 7.5 %collective-permute-done.4 = bf16[256,1024]{1,0:T(8,128)(2,1)} collective-permute-done((bf16[256,1024]{1,0:T(8,128)(2,1)}, bf16[256,1024]{1,0:T(8,128)(2,1)}, u32[]{:S(2)}, u32[]{:S(2)}) %collective-permute-start.4) | collective-permute-done | bytes 524320 | tf_op jit(solution)/shard_map/ppermute | solution.py:26
  393.8 56.8 %while.31 = (s32[]{:T(128)}, f32[1,1024,4,64]{1,3,2,0:T(8,128)S(1)}, f32[1,1024,4,64]{1,3,2,0:T(8,128)}, bf16[2,512,4,64]{1,0,3,2:T(2,128)(2,1)}, s32[2]{0:T(128...) while((s32[]{:T(128)}, ...), condition=%wide.region_17.18_spmd, body=%wide.region_14.17_spmd.sunk | while | flops 1376798720 | bytes 76885448 | solution.py:203
  412.2 9.9 %dynamic_update_slice.31 = bf16[2,512,4,64]{1,0,3,2:T(2,128)(2,1)} dynamic-update-slice(bf16[2,512,4,64]{1,0,3,2:T(2,128)(2,1)} %get-tuple-element.503, bf16[1,512,4,64]{1,0,3,2:T(2,128)(2,1)} %copy.86, s32[]{:T(128)S(6)} %copy.108, s32[]{:T(128)} %constant.230.clone.1..sunk.1, s32[]{:T(128)} %constant.230.clone.1..sunk.1, s32[]{:T(128)} %constant.230.clone.1..sunk.1) | dynamic-update-slice | bytes 524292 | tf_op jit(solution)/shard_map/while/body/jit(dynamic_update_index_in_dim)/dynamic_update_slice | solution.py:203
  440.5 9.9 %dynamic_update_slice.31 = bf16[2,512,4,64]{1,0,3,2:T(2,128)(2,1)} dynamic-update-slice(bf16[2,512,4,64]{1,0,3,2:T(2,128)(2,1)} %get-tuple-element.503, bf16[1,512,4,64]{1,0,3,2:T(2,128)(2,1)} %copy.86, s32[]{:T(128)S(6)} %copy.108, s32[]{:T(128)} %constant.230.clone.1..sunk.1, s32[]{:T(128)} %constant.230.clone.1..sunk.1, s32[]{:T(128)} %constant.230.clone.1..sunk.1) | dynamic-update-slice | bytes 524292 | tf_op jit(solution)/shard_map/while/body/jit(dynamic_update_index_in_dim)/dynamic_update_slice | solution.py:203
  464.4 7.0 %convolution_convert_fusion.3 = bf16[1024,1024]{1,0:T(8,128)(2,1)} fusion(bf16[1024,1024]{1,0:T(8,128)(2,1)} %all-gather.16.cloned.1.call-done, f32[1024,1024]{1,0:T(8,128)} %fusion.78, f32[1024]{0:T(1024)S(1)} %reshape.375), kind=kOutput, calls=%fused_computation.89 | convolution fusion | flops 2159017984 | bytes 8392704 | tf_op jit(solution)/shard_map/dot_general | solution.py:78
  478.5 22.5 %all-reduce.16 = (bf16[32,16]{1,0:T(8,128)(2,1)S(1)}, bf16[64,16]{1,0:T(8,128)(2,1)S(1)}) all-reduce(bf16[32,16]{1,0:T(8,128)(2,1)S(1)} %convert_element_type.163, bf16[64,16]{1,0:T(8,128)(2,1)S(1)} %convert_element_type.169), channel_id=9, replica_groups=mesh['dp'=8,'tensor'=4] {'dp'}, use_global_device_ids=true, to_apply=%region_27.28.clone | all-reduce | flops 1536 | bytes 6144
  507.0 43.3 %reduce-scatter.21.cloned.1.call-done = bf16[256,1024]{1,0:T(8,128)(2,1)} async-done(((bf16[1024,1024]{1,0:T(8,128)(2,1)}), bf16[256,1024]{1,0:T(8,128)(2,1)}) %reduce-scatter.21.cloned.1.call-update) | async-done | bytes 524304 | tf_op jit(solution)/shard_map/reduce_scatter | solution.py:93
  551.9 43.7 %all-reduce.14 = (f32[1024]{0:T(1024)S(1)}, f32[1024]{0:T(1024)S(1)}, f32[1024]{0:T(1024)S(1)}, f32[1024]{0:T(1024)S(1)}, f32[1024]{0:T(1024)S(1)}, /*index=5*/f32[1024]{0:T(1024)S(1)}, f32[1024]{0:T(1024)S(1)}) all-reduce(f32[1024]{0:T(1024)S(1)} %dynamic-update-slice.5, ...), channel_id=1, replica_groups=mesh['dp'=8,'tensor'=4] {'dp','tensor'}, use_global_device_ids=true, to_apply=%add.5 | all-reduce | flops 7168 | bytes 57344
  (234 shorter events, 156.9 us)
Async XLA Ops:
  7.2 69.9 %all-gather.10.cloned.1.call-start = ((), (), s32[]{:S(2)}) async-start(), calls=%async_computation.9 | async-start | bytes 1769472 | tf_op jit(solution)/shard_map/all_gather | solution.py:236
  7.9 94.0 %all-gather.8.cloned.1.call-start = ((), (), s32[]{:S(2)}) async-start(), calls=%async_computation.8 | async-start | bytes 2621440 | tf_op jit(solution)/shard_map/all_gather | solution.py:68
  58.4 114.3 %reduce-scatter.15.cloned.1.call-start = ((), (), s32[]{:S(2)}) async-start(), calls=%async_computation.10 | async-start | bytes 2621440 | tf_op jit(solution)/shard_map/reduce_scatter | solution.py:80
  129.7 92.6 %all-gather.14.cloned.1.call-start = ((), (), s32[]{:S(2)}) async-start(), calls=%async_computation.12 | async-start | bytes 2359296 | tf_op jit(solution)/shard_map/all_gather | solution.py:241
  130.2 118.5 %all-gather.12.cloned.1.call-start = ((), (), s32[]{:S(2)}) async-start(), calls=%async_computation.11 | async-start | bytes 2621440 | tf_op jit(solution)/shard_map/all_gather | solution.py:68
  177.6 101.3 %all-gather.16.cloned.1.call-start = ((), (), s32[]{:S(2)}) async-start(), calls=%async_computation.13 | async-start | bytes 2359296 | tf_op jit(solution)/shard_map/all_gather | solution.py:243
  178.2 158.6 %reduce-scatter.19.cloned.1.call-start = ((), (), s32[]{:S(2)}) async-start(), calls=%async_computation.15 | async-start | bytes 2621440 | tf_op jit(solution)/shard_map/reduce_scatter | solution.py:93
  178.2 23.6 %collective-permute-start = (bf16[256,1024]{1,0:T(8,128)(2,1)S(1)}, bf16[256,1024]{1,0:T(8,128)(2,1)}, u32[]{:S(2)}, u32[]{:S(2)}) collective-permute-start(bf16[256,1024]{1,0:T(8,128)(2,1)S(1)} %copy-done.9), channel_id=1, source_target_pairs={{0,1},{1,2},{2,3},{3,0},{4,5},{5,6},{6,7},{7,4},{8,9},{9,10},{10,1... | collective-permute-start | bytes 1572872 | tf_op jit(solution)/shard_map/ppermute | solution.py:26
  179.8 34.2 %collective-permute-start.2 = (bf16[256,1024]{1,0:T(8,128)(2,1)S(1)}, bf16[256,1024]{1,0:T(8,128)(2,1)}, u32[]{:S(2)}, u32[]{:S(2)}) collective-permute-start(bf16[256,1024]{1,0:T(8,128)(2,1)S(1)} %copy-done.9), channel_id=1, source_target_pairs={{1,0},{2,1},{3,2},{0,3},{5,4},{6,5},{7,6},{4,7},{9,8},{10,9},{11,1... | collective-permute-start | bytes 1572872 | tf_op jit(solution)/shard_map/ppermute | solution.py:28
  201.8 13.9 %collective-permute-start.1 = (bf16[256,1024]{1,0:T(8,128)(2,1)}, bf16[256,1024]{1,0:T(8,128)(2,1)}, u32[]{:S(2)}, u32[]{:S(2)}) collective-permute-start(bf16[256,1024]{1,0:T(8,128)(2,1)} %collective-permute-done), channel_id=1, source_target_pairs={{0,1},{1,2},{2,3},{3,0},{4,5},{5,6},{6,7},{7,4},{8,9},{9,10},{10,1... | collective-permute-start | bytes 1572872 | tf_op jit(solution)/shard_map/ppermute | solution.py:26
  293.6 179.5 %reduce-scatter.29.cloned.1.call-start = ((), (), s32[]{:S(2)}) async-start(), calls=%async_computation.20 | async-start | bytes 2359296
  305.0 170.1 %reduce-scatter.25.cloned.1.call-start = ((), (), s32[]{:S(2)}) async-start(), calls=%async_computation.18 | async-start | bytes 2359296 | tf_op jit(solution)/shard_map/reduce_scatter | solution.py:284
  311.1 191.4 %reduce-scatter.27.cloned.1.call-start = ((), (), s32[]{:S(2)}) async-start(), calls=%async_computation.19 | async-start | bytes 589824
  341.5 23.7 %collective-permute-start.3 = (bf16[256,1024]{1,0:T(8,128)(2,1)S(1)}, bf16[256,1024]{1,0:T(8,128)(2,1)}, u32[]{:S(2)}, u32[]{:S(2)}) collective-permute-start(bf16[256,1024]{1,0:T(8,128)(2,1)S(1)} %convert_element_type.154), channel_id=1, source_target_pairs={{0,1},{1,2},{2,3},{3,0},{4,5},{5,6},{6,7},{7,4},{8,9},{9,10},{10,1... | collective-permute-start | bytes 1572872 | tf_op jit(solution)/shard_map/ppermute | solution.py:26
  343.1 26.5 %collective-permute-start.5 = (bf16[256,1024]{1,0:T(8,128)(2,1)S(1)}, bf16[256,1024]{1,0:T(8,128)(2,1)}, u32[]{:S(2)}, u32[]{:S(2)}) collective-permute-start(bf16[256,1024]{1,0:T(8,128)(2,1)S(1)} %convert_element_type.154), channel_id=1, source_target_pairs={{1,0},{2,1},{3,2},{0,3},{5,4},{6,5},{7,6},{4,7},{9,8},{10,9},{11,1... | collective-permute-start | bytes 1572872 | tf_op jit(solution)/shard_map/ppermute | solution.py:28
  365.2 11.9 %collective-permute-start.4 = (bf16[256,1024]{1,0:T(8,128)(2,1)}, bf16[256,1024]{1,0:T(8,128)(2,1)}, u32[]{:S(2)}, u32[]{:S(2)}) collective-permute-start(bf16[256,1024]{1,0:T(8,128)(2,1)} %collective-permute-done.3), channel_id=1, source_target_pairs={{0,1},{1,2},{2,3},{3,0},{4,5},{5,6},{6,7},{7,4},{8,9},{9,10},{10,1... | collective-permute-start | bytes 1572872 | tf_op jit(solution)/shard_map/ppermute | solution.py:26
  392.1 113.1 %reduce-scatter.23.cloned.1.call-start = ((), (), s32[]{:S(2)}) async-start(), calls=%async_computation.17 | async-start | bytes 1769472 | tf_op jit(solution)/shard_map/reduce_scatter | solution.py:319
  459.2 91.1 %reduce-scatter.21.cloned.1.call-start = ((), (), s32[]{:S(2)}) async-start(), calls=%async_computation.16 | async-start | bytes 2621440 | tf_op jit(solution)/shard_map/reduce_scatter | solution.py:93
  464.3 134.8 %reduce-scatter.17.cloned.1.call-start = ((), (), s32[]{:S(2)}) async-start(), calls=%async_computation.14 | async-start | bytes 2621440 | tf_op jit(solution)/shard_map/reduce_scatter | solution.py:80
  471.4 78.9 %copy-start.13 = (f32[1024]{0:T(1024)S(1)}, f32[1024]{0:T(1024)}, u32[]{:S(2)}) copy-start(f32[1024]{0:T(1024)} %copy-done.12) | copy-start | bytes 12292
  471.4 78.9 %copy-start.15 = (f32[256]{0:T(256)S(1)}, f32[256]{0:T(256)}, u32[]{:S(2)}) copy-start(f32[256]{0:T(256)} %copy-done.14) | copy-start | bytes 3076
  471.4 78.9 %copy-start.17 = (f32[256]{0:T(256)S(1)}, f32[256]{0:T(256)}, u32[]{:S(2)}) copy-start(f32[256]{0:T(256)} %copy-done.16) | copy-start | bytes 3076
  471.5 127.7 %copy-start.2 = (bf16[256,1024]{1,0:T(8,128)(2,1)S(1)}, bf16[256,1024]{1,0:T(8,128)(2,1)}, u32[]{:S(2)}) copy-start(bf16[256,1024]{1,0:T(8,128)(2,1)} %reduce-scatter.15.cloned.1.call-done) | copy-start | bytes 1572868
  471.5 127.7 %copy-start.4 = (f32[256,1024]{1,0:T(8,128)S(1)}, f32[256,1024]{1,0:T(8,128)}, u32[]{:S(2)}) copy-start(f32[256,1024]{1,0:T(8,128)} %copy-done.3) | copy-start | bytes 3145732
  (21 other events, 290.6 us)
Sparse Core Ops, SparseCore 0:
  9.9 26.7 all-gather.9
  58.6 43.3 all-gather.7
  129.8 42.9 reduce-scatter.14
  174.5 27.7 all-gather.13
  204.3 44.4 all-gather.11
  250.5 28.3 all-gather.15
  293.7 43.1 reduce-scatter.18
  340.1 41.1 reduce-scatter.28
  384.6 41.1 reduce-scatter.24
  429.3 34.1 reduce-scatter.26
  466.7 38.4 reduce-scatter.22
  507.4 42.8 reduce-scatter.20
  552.6 43.8 reduce-scatter.16
